TPU v7x, 32 devices: a 4x4x1 block of a 4x4x8 slice. The times are simulated.
32 devices in a mesh: dp: 1 (over z), ep: 32 (over y, x, core).
Axes of the slice: x: 4, y: 4, z: 1, core: 2. Of those that a mesh axis runs over, the one named last changes fastest.
The devices are a block of a 4x4x8 slice.
Arguments:
- hidden_in: bfloat16 [3072, 2048], P(('dp', 'ep'))
- norm_gain: float32 [2048], replicated
- router_w: float32 [64, 2048], replicated
- w_gate: bfloat16 [64, 2048, 1408], P('ep')
- w_up: bfloat16 [64, 2048, 1408], P('ep')
- w_down: bfloat16 [64, 1408, 2048], P('ep')
- ws_gate: bfloat16 [2048, 2816], replicated
- ws_up: bfloat16 [2048, 2816], replicated
- ws_down: bfloat16 [2816, 2048], replicated
- expert_ids: int32 [3072, 6], P(('dp', 'ep'))
Outputs:
- output: bfloat16 [3072, 2048], P(('dp', 'ep'))
All inputs are finite; a program needn't handle non-finite values.
Results may differ from a plain program's by a relative error of at most 0.00429402.
Values are sent between devices in bfloat16 or wider.
A program may use at most 768 MiB of HBM per device.

v0:
```python
import jax
import jax.numpy as jnp
from jax import lax
from jax.sharding import PartitionSpec as P

NORM_EPS = 1e-6
ROUTE_SCALE = 2.5
GROUPS = 8
GROUP_LIMIT = 4


def rms_norm(x_rows, norm_gain):
    x_f32 = x_rows.astype(jnp.float32)
    inv_rms = lax.rsqrt(jnp.mean(x_f32 * x_f32, axis=-1, keepdims=True) + NORM_EPS)
    return (x_f32 * inv_rms * norm_gain).astype(jnp.bfloat16)


def route_gates(x_norm, router_w, expert_ids):
    logits = jnp.einsum("td,nd->tn", x_norm.astype(jnp.float32), router_w, precision=lax.Precision.HIGHEST, preferred_element_type=jnp.float32)
    picked = jnp.take_along_axis(jax.nn.sigmoid(logits), expert_ids, axis=1)
    return ROUTE_SCALE * picked / jnp.sum(picked, axis=1, keepdims=True)


def swiglu(tok_rows, gate_mat, up_mat, down_mat):
    h_gate = jnp.dot(tok_rows, gate_mat, preferred_element_type=jnp.float32)
    h_up = jnp.dot(tok_rows, up_mat, preferred_element_type=jnp.float32)
    hidden = (jax.nn.silu(h_gate) * h_up).astype(jnp.bfloat16)
    return jnp.dot(hidden, down_mat, preferred_element_type=jnp.float32).astype(jnp.bfloat16)


def expert_stack(expert_in, w_gate, w_up, w_down):
    h_gate = jnp.einsum("ecd,edi->eci", expert_in, w_gate, preferred_element_type=jnp.float32)
    h_up = jnp.einsum("ecd,edi->eci", expert_in, w_up, preferred_element_type=jnp.float32)
    hidden = (jax.nn.silu(h_gate) * h_up).astype(jnp.bfloat16)
    return jnp.einsum("eci,eid->ecd", hidden, w_down, preferred_element_type=jnp.float32).astype(jnp.bfloat16)


def solution(mesh):
    ep_size = mesh.shape["ep"]

    def local_block(hidden_in, norm_gain, router_w, w_gate, w_up, w_down, ws_gate, ws_up, ws_down, expert_ids):
        tok_dev, top_k = expert_ids.shape
        model_dim = hidden_in.shape[1]
        exp_dev = w_gate.shape[0]
        pair_cap = GROUPS * ((top_k + GROUP_LIMIT - 1) // GROUP_LIMIT) * tok_dev // ep_size
        recv_cap = pair_cap * ep_size
        exp_cap = recv_cap // exp_dev
        x_norm = rms_norm(hidden_in, norm_gain)
        gate_vals = route_gates(x_norm, router_w, expert_ids)
        shared_out = swiglu(x_norm, ws_gate, ws_up, ws_down)

        flat_ids = expert_ids.reshape(-1)
        dest_dev = flat_ids // exp_dev
        dest_hot = (dest_dev[:, None] == jnp.arange(ep_size, dtype=jnp.int32)[None, :]).astype(jnp.int32)
        dest_rank = jnp.sum((jnp.cumsum(dest_hot, axis=0) - 1) * dest_hot, axis=1)
        send_slot = dest_dev * pair_cap + dest_rank
        pair_tok = jnp.arange(tok_dev * top_k, dtype=jnp.int32) // top_k
        slot_tok = jnp.full((recv_cap,), tok_dev, jnp.int32).at[send_slot].set(pair_tok)
        slot_exp = jnp.full((recv_cap,), -1, jnp.int32).at[send_slot].set(flat_ids % exp_dev)
        send_rows = jnp.take(x_norm, slot_tok, axis=0, mode="fill", fill_value=0)
        recv_rows = lax.all_to_all(send_rows, "ep", 0, 0, tiled=True)
        recv_exp = lax.all_to_all(slot_exp, "ep", 0, 0, tiled=True)

        exp_hot = (recv_exp[:, None] == jnp.arange(exp_dev, dtype=jnp.int32)[None, :]).astype(jnp.int32)
        exp_rank = jnp.sum((jnp.cumsum(exp_hot, axis=0) - 1) * exp_hot, axis=1)
        buf_slot = jnp.where(recv_exp >= 0, recv_exp * exp_cap + exp_rank, recv_cap)
        buf_row = jnp.full((recv_cap,), recv_cap, jnp.int32).at[buf_slot].set(jnp.arange(recv_cap, dtype=jnp.int32), mode="drop")
        expert_in = jnp.take(recv_rows, buf_row, axis=0, mode="fill", fill_value=0).reshape(exp_dev, exp_cap, model_dim)
        expert_out = expert_stack(expert_in, w_gate, w_up, w_down).reshape(recv_cap, model_dim)
        back_rows = jnp.take(expert_out, buf_slot, axis=0, mode="fill", fill_value=0)
        returned = lax.all_to_all(back_rows, "ep", 0, 0, tiled=True)

        pair_out = jnp.take(returned, send_slot, axis=0).reshape(tok_dev, top_k, model_dim)
        routed = jnp.sum(gate_vals[:, :, None] * pair_out.astype(jnp.float32), axis=1)
        return (hidden_in.astype(jnp.float32) + shared_out.astype(jnp.float32) + routed).astype(jnp.bfloat16)

    row_spec = P(("dp", "ep"), None)
    in_specs = (row_spec, P(), P(), P("ep"), P("ep"), P("ep"), P(), P(), P(), row_spec)
    return jax.shard_map(local_block, mesh=mesh, in_specs=in_specs, out_specs=row_spec, check_vma=False)
```

profile of v0, /device:TPU:103, one launch (start us, length us, event | category | flops | bytes accessed | tf_op | source)
XLA Modules:
  0.0 333.6 jit_solution(13183069569119563150)
XLA Ops:
  0.0 0.8 copy.49
  0.8 0.1 reshape.249
  1.0 0.1 reshape.252
  1.2 1.5 reduce-window.14
  2.6 0.3 slice_reduce_fusion
  2.9 0.1 bitcast_bitcast_fusion
  3.1 4.1 %scatter_custom_fusion.1 = s32[1536]{0:T(1024)S(1)} fusion(s32[576]{0:T(1024)S(1)} %fusion.32, s32[576]{0:T(1024)S(1)} %get-tuple-element.10, s32[]{:T(128)} %constant.116.clone.1), kind=kCustom, calls=%fused_computation.88 | custom fusion | bytes 6148 | tf_op jit(solution)/shard_map/scatter | solution.py:59
  7.2 0.7 all_to_all.22
  7.9 8.0 %all-to-all-start.1 = ((s32[32,48,1]{1,2,0:T(1,128)}), s32[32,48,1]{1,2,0:T(1,128)S(1)}, u32[]{:S(2)}, u32[]{:S(2)}) async-start(s32[32,48,1]{1,2,0:T(1,128)} %all_to_all.22), calls=%async_computation.1 | async-start | bytes 32768 | tf_op jit(solution)/shard_map/all_to_all | solution.py:62
  15.9 4.1 %scatter_custom_fusion = s32[1536]{0:T(1024)S(1)} fusion(s32[576]{0:T(1024)S(1)} %fusion.32, s32[576]{0:T(1024)S(1)} %add_select_fusion.1, s32[]{:T(128)} %constant.121.clone.1), kind=kCustom, calls=%fused_computation.92 | custom fusion | bytes 6148 | tf_op jit(solution)/shard_map/scatter | solution.py:58
  20.1 1.2 fusion.8
  21.2 0.1 broadcast_in_dim.59
  21.3 1.2 fusion.10
  22.5 7.1 %gather_fusion = bf16[1536,2048]{1,0:T(8,128)(2,1)} fusion(bf16[96,2048]{1,0:T(8,128)(2,1)S(1)} %fusion.10, s32[2048]{0:T(1024)S(1)} %pad_clamp_fusion.2), kind=kCustom, calls=%fused_computation.2 | custom fusion | bytes 12589056 | tf_op jit(solution)/shard_map/jit(_take)/gather | solution.py:60
  29.6 5.9 %broadcast_select_fusion.2 = bf16[32,48,2048]{2,1,0:T(8,128)(2,1)} fusion(bf16[32,48,2048]{2,1,0:T(8,128)(2,1)} %bitcast.56, pred[32,48]{1,0:T(8,128)(4,1)S(1)} %broadcast_in_dim.59), kind=kLoop, calls=%fused_computation.12 | loop fusion | flops 3145728 | bytes 12584448 | tf_op jit(solution)/shard_map/jit(_take)/select_n | solution.py:60
  35.6 6.3 %all-to-all-start = ((bf16[32,48,2048]{2,1,0:T(8,128)(2,1)}), bf16[32,48,2048]{2,1,0:T(8,128)(2,1)}, u32[]{:S(2)}, u32[]{:S(2)}) async-start(bf16[32,48,2048]{2,1,0:T(8,128)(2,1)} %broadcast_select_fusion.2), calls=%async_computation | async-start | bytes 12582912 | tf_op jit(solution)/shard_map/all_to_all | solution.py:61
  42.0 0.6 reduce-window.16
  42.5 0.2 slice_reduce_fusion.1
  42.7 0.2 reduce-window.19
  42.9 0.5 broadcast.352
  43.4 0.7 fusion.40
  44.2 0.1 eq.53
  44.3 0.1 mul.112
  44.4 0.1 ge.48
  44.7 6.2 %scatter_custom_fusion.2 = s32[1536]{0:T(1024)S(1)} fusion(s32[1536]{0:T(1024)S(1)} %fusion.16, s32[1536]{0:T(1024)S(1)} %iota.20, s32[]{:T(128)} %constant.119.clone.1), kind=kCustom, calls=%fused_computation.90 | custom fusion | bytes 6148 | tf_op jit(solution)/shard_map/scatter | solution.py:67
  50.9 75.4 %all-to-all-done = bf16[32,48,2048]{2,1,0:T(8,128)(2,1)} async-done(((bf16[32,48,2048]{2,1,0:T(8,128)(2,1)}), bf16[32,48,2048]{2,1,0:T(8,128)(2,1)}, u32[]{:S(2)}, u32[]{:S(2)}) %all-to-all-start) | async-done | bytes 6291488 | tf_op jit(solution)/shard_map/all_to_all | solution.py:61
  126.3 16.5 %gather_fusion.3 = bf16[1536,2048]{1,0:T(8,128)(2,1)} fusion(bf16[1536,2048]{1,0:T(8,128)(2,1)} %bitcast.4, s32[2048]{0:T(1024)S(1)} %pad_clamp_fusion.1), kind=kCustom, calls=%fused_computation.clone | custom fusion | bytes 12589056 | tf_op jit(solution)/shard_map/jit(_take)/gather | solution.py:68
  142.8 3.3 broadcast_select_fusion.1
  146.1 2.6 copy-done.2
  148.7 14.7 %fusion.41 = f32[2,768,1408]{2,1,0:T(8,128)} fusion(bf16[2,768,2048]{2,1,0:T(8,128)(2,1)S(1)} %bitcast.57, bf16[2,2048,1408]{2,1,0:T(8,128)(2,1)} %param.15), kind=kOutput, calls=%fused_computation.109 | convolution fusion | flops 8858370048 | bytes 26476544 | tf_op jit(solution)/shard_map/ecd,edi->eci/dot_general | solution.py:32
  163.4 28.8 %convolution_convert_fusion = bf16[2,768,2048]{2,1,0:T(8,128)(2,1)} fusion(bf16[2,1408,2048]{2,1,0:T(8,128)(2,1)} %param.17, f32[2,768,1408]{2,1,0:T(8,128)} %fusion.41, bf16[2,768,2048]{2,1,0:T(8,128)(2,1)} %bitcast.58, bf16[2,2048,1408]{2,1,0:T(8,128)(2,1)} %param.16), kind=kOutput, calls=%fused_computation.13 | convolution fusion | flops 17732861952 | bytes 44302336 | tf_op jit(solution)/shard_map/eci,eid->ecd/dot_general | solution.py:35
  192.2 16.3 %gather_fusion.4 = bf16[1536,2048]{1,0:T(8,128)(2,1)} fusion(bf16[1536,2048]{1,0:T(8,128)(2,1)} %bitcast.54, s32[2048]{0:T(1024)S(1)} %pad_clamp_fusion), kind=kCustom, calls=%fused_computation.1.clone | custom fusion | bytes 12589056 | tf_op jit(solution)/shard_map/jit(_take)/gather | solution.py:70
  208.6 5.9 %broadcast_select_fusion = bf16[1536,2048]{1,0:T(8,128)(2,1)} fusion(bf16[1536,2048]{1,0:T(8,128)(2,1)} %gather_fusion.4, pred[1536]{0:T(1024)(128)(4,1)S(1)} %get-tuple-element.8), kind=kLoop, calls=%fused_computation.10 | loop fusion | flops 3145728 | bytes 12584448 | tf_op jit(solution)/shard_map/jit(_take)/select_n | solution.py:70
  214.4 4.0 %all-to-all-start.2 = ((bf16[32,48,2048]{2,1,0:T(8,128)(2,1)}), bf16[32,48,2048]{2,1,0:T(8,128)(2,1)}, u32[]{:S(2)}, u32[]{:S(2)}) async-start(bf16[32,48,2048]{2,1,0:T(8,128)(2,1)} %bitcast.55), calls=%async_computation.2 | async-start | bytes 12582912 | tf_op jit(solution)/shard_map/all_to_all | solution.py:71
  218.5 0.1 reduce_sum.54
  218.7 0.1 copy.53
  218.9 0.1 copy.46
  219.0 0.1 reshape.289
  219.1 0.6 fusion.7
  219.7 4.0 %gather_fusion.2 = f32[576]{0:T(1024)S(1)} fusion(f32[96,64]{0,1:T(8,128)S(1)} %fusion.7, s32[576]{0:T(1024)S(1)} %reshape.289), kind=kCustom, calls=%fused_computation.4 | custom fusion | bytes 9216 | tf_op jit(solution)/shard_map/jit(take_along_axis)/gather | solution.py:20
  223.8 0.1 reshape.292
  224.0 0.1 copy.48
  224.1 7.3 %fusion.38 = f32[96,2816]{1,0:T(8,128)} fusion(bf16[2048,2816]{1,0:T(8,128)(2,1)} %param.18, bf16[96,2048]{1,0:T(8,128)(2,1)S(1)} %copy-done.1, f32[2048]{0:T(1024)S(1)} %copy-done.3, f32[96]{0:T(128)S(1)} %add_rsqrt_fusion), kind=kOutput, calls=%fused_computation.107 | convolution fusion | flops 1108082688 | bytes 13017472 | tf_op jit(solution)/shard_map/dot_general | solution.py:25
  231.5 71.4 %all-to-all-done.2 = bf16[32,48,2048]{2,1,0:T(8,128)(2,1)} async-done(((bf16[32,48,2048]{2,1,0:T(8,128)(2,1)}), bf16[32,48,2048]{2,1,0:T(8,128)(2,1)}, u32[]{:S(2)}, u32[]{:S(2)}) %all-to-all-start.2) | async-done | bytes 6291488 | tf_op jit(solution)/shard_map/all_to_all | solution.py:71
  302.9 9.9 %gather_fusion.1 = bf16[576,2048]{1,0:T(8,128)(2,1)S(1)} fusion(bf16[1536,2048]{1,0:T(8,128)(2,1)} %bitcast.8, s32[1024]{0:T(1024)S(1)} %pad_clamp_fusion.3), kind=kCustom, calls=%fused_computation.3 | custom fusion | bytes 4720896 | tf_op jit(solution)/shard_map/jit(_take)/gather | solution.py:73
  312.8 2.6 gather.23
  315.4 5.3 %multiply_reduce_fusion = f32[96,2048]{1,0:T(8,128)S(1)} fusion(bf16[96,6,2048]{2,1,0:T(8,128)(2,1)} %gather.23, f32[96,6]{1,0:T(8,128)S(1)} %copy.48, pred[96,6]{1,0:T(8,128)(4,1)S(1)} %copy.53), kind=kLoop, calls=%fused_computation.9 | loop fusion | flops 4521984 | bytes 3148608 | tf_op jit(solution)/shard_map/reduce_sum | solution.py:74
  320.7 12.7 %fusion.4 = bf16[96,2048]{1,0:T(8,128)(2,1)} fusion(f32[96,2048]{1,0:T(8,128)S(1)} %multiply_reduce_fusion, bf16[2816,2048]{1,0:T(8,128)(2,1)} %param.20, bf16[96,2048]{1,0:T(8,128)(2,1)S(1)} %copy-done.1, bf16[2048,2816]{1,0:T(8,128)(2,1)} %param.19, f32[96,2816]{1,0:T(8,128)} %fusion.38, f32[2048]{0:T(1024)S(1)} %copy-done.3, f32[96]{0:T(128)S(1)} %add_rsqrt_fusion), kind=kOutput, calls=%fused_computation.20 | convolution fusion | flops 2218180608 | bytes 25731456 | tf_op jit(solution)/shard_map/dot_general | solution.py:28
  (40 shorter events, 0.7 us)
Async XLA Ops:
  0.0 219.1 %copy-start = (f32[64,2048]{1,0:T(8,128)S(1)}, f32[64,2048]{1,0:T(8,128)}, u32[]{:S(2)}) copy-start(f32[64,2048]{1,0:T(8,128)} %param.14) | copy-start | bytes 1572868
  7.9 27.7 %all-to-all-start.1 = ((s32[32,48,1]{1,2,0:T(1,128)}), s32[32,48,1]{1,2,0:T(1,128)S(1)}, u32[]{:S(2)}, u32[]{:S(2)}) async-start(s32[32,48,1]{1,2,0:T(1,128)} %all_to_all.22), calls=%async_computation.1 | async-start | bytes 32768 | tf_op jit(solution)/shard_map/all_to_all | solution.py:62
  35.6 90.7 %all-to-all-start = ((bf16[32,48,2048]{2,1,0:T(8,128)(2,1)}), bf16[32,48,2048]{2,1,0:T(8,128)(2,1)}, u32[]{:S(2)}, u32[]{:S(2)}) async-start(bf16[32,48,2048]{2,1,0:T(8,128)(2,1)} %broadcast_select_fusion.2), calls=%async_computation | async-start | bytes 12582912 | tf_op jit(solution)/shard_map/all_to_all | solution.py:61
  146.1 2.6 copy-start.2
  214.4 4.3 %copy-start.4 = (s32[96,6]{0,1:T(8,128)S(1)}, s32[96,6]{0,1:T(8,128)}, u32[]{:S(2)}) copy-start(s32[96,6]{0,1:T(8,128)} %param.21) | copy-start | bytes 6916
  214.4 4.7 %copy-start.1 = (bf16[96,2048]{1,0:T(8,128)(2,1)S(1)}, bf16[96,2048]{1,0:T(8,128)(2,1)}, u32[]{:S(2)}) copy-start(bf16[96,2048]{1,0:T(8,128)(2,1)} %param.12) | copy-start | bytes 1179652
  214.4 4.7 %copy-start.3 = (f32[2048]{0:T(1024)S(1)}, f32[2048]{0:T(1024)}, u32[]{:S(2)}) copy-start(f32[2048]{0:T(1024)} %param.13) | copy-start | bytes 24580
  214.4 88.4 %all-to-all-start.2 = ((bf16[32,48,2048]{2,1,0:T(8,128)(2,1)}), bf16[32,48,2048]{2,1,0:T(8,128)(2,1)}, u32[]{:S(2)}, u32[]{:S(2)}) async-start(bf16[32,48,2048]{2,1,0:T(8,128)(2,1)} %bitcast.55), calls=%async_computation.2 | async-start | bytes 12582912 | tf_op jit(solution)/shard_map/all_to_all | solution.py:71
where the time goes:
time: 340 us; the launch traced here: 334 us
  waiting for transfers between devices  147 us (43%)
  local copies, waits for them, and re-layouts  77.5 us (23%)
  matrix products  64.2 us (19%)
  other arithmetic  26.3 us (8%)
  starting transfers between devices  18.3 us (5%)
    all_to_all x1, waiting for transfers between devices, local_block(): recv_rows = lax.all_to_all(send_rows, 'ep', 0, 0, tiled=True)  75.4 us
    all_to_all x1, waiting for transfers between devices, local_block(): returned = lax.all_to_all(back_rows, 'ep', 0, 0, tiled=True)  71.4 us
    dot_general x1, matrix products, expert_stack(): jnp.einsum('eci,eid->ecd', hidden, w_down, preferred_element_type=jnp.flo...  28.8 us
    gather x1, local copies, waits for them, and re-layouts, local_block(): jnp.take(recv_rows, buf_row, axis=0, mode='fill', fill_value=0)  16.5 us
    gather x1, local copies, waits for them, and re-layouts, local_block(): jnp.take(expert_out, buf_slot, axis=0, mode='fill', fill_value=0)  16.3 us
    dot_general x1, matrix products, expert_stack(): jnp.einsum('ecd,edi->eci', expert_in, w_gate, preferred_element_type=jnp....  14.7 us
    dot_general x1, matrix products, swiglu(): jnp.dot(hidden, down_mat, preferred_element_type=jnp.float32)  12.7 us
    gather x2, local copies, waits for them, and re-layouts, local_block(): jnp.take(returned, send_slot, axis=0).reshape(tok_dev, top_k, model_dim)  12.5 us
  transfers between devices with their start and end apart: 3, of which 2 were waited for; matrix products, arithmetic and copies ran while one was open for 12% of the time, Pallas kernels for 0%

commit v1 on v0

v1 whole, which is shorter than its diff:
```python
import functools
import math

import jax
import jax.numpy as jnp
from jax import lax
from jax.experimental import pallas as pl
from jax.experimental.pallas import tpu as pltpu
from jax.sharding import PartitionSpec as P

NORM_EPS = 1e-6
ROUTE_SCALE = 2.5
GROUPS = 8
GROUP_LIMIT = 4
MESH = pl.DeviceIdType.MESH
F32 = jnp.float32
BF16 = jnp.bfloat16
LINE = (0, -1, 1, 2)
CHUNKS = (
    ((0, 0), (1, 0), (-1, 0), (0, 1)),
    ((0, -1), (1, 1), (-1, 1), (1, -1)),
    ((-1, -1), (2, 0), (0, 2), (2, 1)),
    ((2, -1), (1, 2), (-1, 2), (2, 2)),
)
NT = (((1,), (1,)), ((), ()))


def split3(value):
    hi = value.astype(BF16)
    rest = value - hi.astype(F32)
    mid = rest.astype(BF16)
    lo = (rest - mid.astype(F32)).astype(BF16)
    return hi, mid, lo


def dot(a, b, dims=None):
    dims = (((1,), (0,)), ((), ())) if dims is None else dims
    return lax.dot_general(a, b, dims, preferred_element_type=F32)


def moe_kernel(
    side, cap,
    x_ref, gain_ref, router_ref, ids_ref, wg_hbm, wu_hbm, wd_hbm, sg_hbm, su_hbm, sd_hbm,
    out_ref, recv_hbm,
    wg, wu, wd, xall, xn, outb, xs, h, mask, acc, hs, meta, meta_in,
    w_sem, s_sem, ag_send, ag_recv, d2d_send, d2d_recv, meta_send, meta_recv, ret_send, ret_recv, load_sem,
):
    ep = 2 * side * side
    tok, dim = x_ref.shape
    inter = wg.shape[2]
    sinter = hs.shape[1]
    quarter = dim // 4
    lanes = meta.shape[2]
    nexp = router_ref.shape[0]
    me = lax.axis_index("ep")
    core = lax.rem(me, 2)
    chip = lax.div(me, 2)
    my_x = lax.rem(chip, side)
    my_y = lax.div(chip, side)

    def at_chip(dx, dy, dc=0):
        col = lax.rem(my_x + (dx + side), side)
        row = lax.rem(my_y + (dy + side), side)
        return (row * side + col) * 2 + (lax.rem(core + dc, 2) if dc else core)

    def at(half, da, db, dc=0):
        return at_chip(da, db, dc) if half == 0 else at_chip(db, da, dc)

    def rows(src, first, count):
        return xall.at[pl.ds(pl.multiple_of((src * 4 + first) * tok, tok), count * tok)]

    barrier = pltpu.get_barrier_semaphore()

    def greet(k, carry):
        pl.semaphore_signal(barrier, inc=1, device_id={"ep": lax.rem(me + k, ep)}, device_id_type=MESH)
        return carry

    lax.fori_loop(1, ep, greet, 0)
    weight_copies = []
    for i, (src, dst) in enumerate(((wg_hbm, wg), (wu_hbm, wu))):
        for e in range(2):
            weight_copies.append(pltpu.make_async_copy(src.at[e], dst.at[e], w_sem.at[i * 2 + e]))
    for e in range(2):
        weight_copies.append(
            pltpu.make_async_copy(wd_hbm.at[pl.ds(e * inter, inter)], wd.at[pl.ds(e * inter, inter)], w_sem.at[4 + e])
        )
    for copy in weight_copies:
        copy.start()

    x = x_ref[...].astype(F32)
    inv = lax.rsqrt(jnp.mean(x * x, axis=1, keepdims=True) + NORM_EPS)
    x_norm = (x * inv * gain_ref[...]).astype(BF16)
    xn[...] = x_norm
    base = pl.multiple_of(me * 4 * tok, tok)
    for q in range(4):
        xall[pl.ds(pl.multiple_of(base + q * tok, tok), tok), :] = x_norm[:, q * quarter : (q + 1) * quarter]

    ids = ids_ref[...]
    expert = lax.broadcasted_iota(jnp.int32, (nexp, lanes), 0)
    hot = expert == ids[0:1, :]
    top = 6
    for k in range(1, top):
        hot = jnp.logical_or(hot, expert == ids[k : k + 1, :])
    hot = jnp.where(hot, 1.0, 0.0)
    hot_b = hot.astype(BF16)
    upper = lax.broadcasted_iota(jnp.int32, (lanes, lanes), 0) < lax.broadcasted_iota(jnp.int32, (lanes, lanes), 1)
    before = dot(hot_b, jnp.where(upper, 1.0, 0.0).astype(BF16))
    e_row = lax.broadcasted_iota(jnp.int32, (nexp, nexp), 0)
    e_col = lax.broadcasted_iota(jnp.int32, (nexp, nexp), 1)
    same_dev = jnp.where(lax.shift_right_logical(e_row, 1) == lax.shift_right_logical(e_col, 1), 1.0, 0.0).astype(BF16)
    is_odd = jnp.bitwise_and(e_row, 1) == 1
    prev = jnp.where(jnp.logical_and(is_odd, e_col == e_row - 1), 1.0, 0.0).astype(BF16)
    rank = dot(same_dev, before.astype(BF16)) + dot(prev, hot_b)
    rank = jnp.where(hot > 0.5, rank, -1.0)
    r_hi, r_mid, r_lo = split3(router_ref[...])
    logits = dot(r_hi, x_norm, NT) + dot(r_mid, x_norm, NT) + dot(r_lo, x_norm, NT)
    picked = jnp.where(hot[:, :tok] > 0.5, jax.nn.sigmoid(logits), 0.0)
    gates = ROUTE_SCALE * picked / jnp.sum(picked, axis=0, keepdims=True)
    for d in range(ep):
        meta[d, 0:2, :] = rank[2 * d : 2 * d + 2, :]
        meta[d, 2:4, 0:tok] = gates[2 * d : 2 * d + 2, :]

    pl.semaphore_wait(barrier, ep - 1)

    sends = []

    def remote(src, dst, send_sem, recv_sem, target):
        return pltpu.make_async_remote_copy(
            src_ref=src, dst_ref=dst, send_sem=send_sem, recv_sem=recv_sem,
            device_id={"ep": target}, device_id_type=MESH,
        )

    def ag_copy(half, piece, block, first, count, target):
        remote(
            rows(block, first, count), rows(block, first, count), ag_send.at[half, piece], ag_recv.at[half, piece], target
        ).start()
        sends.append((ag_send, half, piece, count))

    def ag_wait(half, piece, block, first, count):
        remote(
            rows(block, first, count), rows(block, first, count), ag_send.at[half, piece], ag_recv.at[half, piece], at(half, 1, 0)
        ).wait_recv()

    def chip_slot(da, db, half):
        dx, dy = (da, db) if half == 0 else (db, da)
        return (dy % side) * side + dx % side

    def swap(half, da, db):
        block = at(half, da, db)
        view = rows(block, 2 * half, 2)
        slot = chip_slot(da, db, half)
        remote(view, view, d2d_send.at[half, slot], d2d_recv.at[half, slot], at_chip(0, 0, 1)).start()
        sends.append((d2d_send, half, slot, 2))

    def second_axis(half, line):
        block = at(half, LINE[line], 0)
        ag_copy(half, 4 + 2 * line, block, 2 * half, 2, at(half, 0, 1))
        ag_copy(half, 5 + 2 * line, block, 2 * half, 2, at(half, 0, -1))

    def first_arrived(half, way):
        off = (-1, 1)[way]
        block = at(half, off, 0)
        ag_wait(half, way, block, 2 * half, 2)
        ag_copy(half, 2 + way, block, 2 * half + way, 1, at(half, -off, 0))
        second_axis(half, 1 + way)
        swap(half, off, 0)

    def first_far_arrived(half):
        block = at(half, 2, 0)
        for way in range(2):
            ag_wait(half, 2 + way, block, 2 * half + way, 1)
        second_axis(half, 3)
        swap(half, 2, 0)

    def second_arrived(half, line, way):
        off = (-1, 1)[way]
        block = at(half, LINE[line], off)
        ag_wait(half, 4 + 2 * line + way, block, 2 * half, 2)
        ag_copy(half, 12 + 2 * line + way, block, 2 * half + way, 1, at(half, 0, -off))
        swap(half, LINE[line], off)

    def second_far_arrived(half, line):
        block = at(half, LINE[line], 2)
        for way in range(2):
            ag_wait(half, 12 + 2 * line + way, block, 2 * half + way, 1)
        swap(half, LINE[line], 2)

    for half in range(2):
        ag_copy(half, 0, me, 2 * half, 2, at(half, 1, 0))
        ag_copy(half, 1, me, 2 * half, 2, at(half, -1, 0))

    def meta_copy(k):
        target = lax.rem(me + k, ep)
        return remote(meta.at[target], meta_in.at[me], meta_send.at[k], meta_recv.at[me], target)

    def send_meta(k, carry):
        meta_copy(k).start()
        return carry

    for half in range(2):
        second_axis(half, 0)
    lax.fori_loop(1, ep, send_meta, 0)
    own_meta = pltpu.make_async_copy(meta.at[me], meta_in.at[me], meta_recv.at[me])
    own_meta.start()
    for half in range(2):
        swap(half, 0, 0)
    for half in range(2):
        for way in range(2):
            first_arrived(half, way)
    for half in range(2):
        for way in range(2):
            second_arrived(half, 0, way)

    def events(*calls):
        return calls

    gate_events = (
        events((first_far_arrived, 0), (first_far_arrived, 1)),
        events((second_arrived, 0, 1, 0), (second_arrived, 1, 1, 0), (second_arrived, 0, 1, 1), (second_arrived, 1, 1, 1)),
        events((second_arrived, 0, 2, 0), (second_arrived, 1, 2, 0), (second_arrived, 0, 2, 1), (second_arrived, 1, 2, 1)),
        events((second_far_arrived, 0, 0), (second_far_arrived, 1, 0)),
        events((second_arrived, 0, 3, 0), (second_arrived, 1, 3, 0), (second_arrived, 0, 3, 1), (second_arrived, 1, 3, 1)),
    )
    down_events = (
        events((second_far_arrived, 0, 1), (second_far_arrived, 1, 1)),
        events((second_far_arrived, 0, 2), (second_far_arrived, 1, 2)),
        events((second_far_arrived, 0, 3), (second_far_arrived, 1, 3)),
    )

    tile = 256
    per = 2 * len(CHUNKS[0])
    full, left = inter // tile, inter % tile
    down_tiles = dim // tile

    def chunk_device(c, j):
        return (*CHUNKS[c][j // 2], j % 2)

    def wait_meta(src):
        remote(meta.at[0], meta_in.at[src], meta_send.at[1], meta_recv.at[src], src).wait_recv()

    def select(c):
        slot_no = lax.broadcasted_iota(jnp.int32, (cap, tok), 0).astype(F32)
        for j in range(per):
            dx, dy, dc = chunk_device(c, j)
            src = at_chip(dx, dy, dc)
            if (dx, dy, dc) == (0, 0, 0):
                own_meta.wait()
            else:
                wait_meta(src)
            if dc:
                for half in range(2):
                    slot = (dy % side) * side + dx % side
                    view = rows(src, 2 * half, 2)
                    remote(view, view, d2d_send.at[half, slot], d2d_recv.at[half, slot], at_chip(0, 0, 1)).wait_recv()
            low = jnp.where(slot_no == meta_in[src, 0:1, 0:tok], 1.0, 0.0)
            high = jnp.where(slot_no == meta_in[src, 1:2, 0:tok], 1.0, 0.0)
            mask[j * cap : (j + 1) * cap, :] = jnp.broadcast_to(jnp.sum(low, axis=1, keepdims=True), (cap, tile))
            pick = (low + high).astype(BF16)
            for q in range(4):
                block = xall[pl.ds(pl.multiple_of((src * 4 + q) * tok, tok), tok), :]
                xs[j * cap : (j + 1) * cap, q * quarter : (q + 1) * quarter] = dot(pick, block).astype(BF16)

    def gated(gate, up, is_low, keep_low):
        keep = is_low > 0.5
        keep = keep if keep_low else jnp.logical_not(keep)
        return jnp.where(keep, jax.nn.silu(gate) * up, 0.0).astype(BF16)

    def gate_up(n, carry):
        cols = pl.ds(pl.multiple_of(n * tile, tile), tile)
        for e in range(2):
            gate = dot(xs[...], wg[e, :, cols])
            up = dot(xs[...], wu[e, :, cols])
            h[:, pl.ds(pl.multiple_of(e * inter + n * tile, 128), tile)] = gated(gate, up, mask[...], e == 0)
        return carry

    def gate_up_left():
        cols = slice(full * tile, inter)
        for e in range(2):
            both = dot(xs[...], jnp.concatenate([wg[e, :, cols], wu[e, :, cols]], axis=1))
            h[:, e * inter + full * tile : (e + 1) * inter] = gated(both[:, :left], both[:, left:], mask[:, :left], e == 0)

    def down(c, n):
        cols = pl.ds(pl.multiple_of(n * tile, tile), tile)
        y = dot(h[...], wd[:, cols]).astype(BF16)
        outb[c * per : (c + 1) * per, :, cols] = y.reshape(per, cap, tile)

    def run_events(n, table):
        for k, calls in enumerate(table):
            if calls:

                @pl.when(n == k)
                def _():
                    for fn, *args in calls:
                        fn(*args)

    ret_copies = []

    def send_back(c):
        for j in range(per):
            dx, dy, dc = chunk_device(c, j)
            block = outb.at[c * per + j]
            if (dx, dy, dc) == (0, 0, 0):
                copy = pltpu.make_async_copy(block, recv_hbm.at[me], ret_recv.at[me])
            else:
                copy = remote(block, recv_hbm.at[me], ret_send.at[c * per + j], ret_recv.at[me], at_chip(dx, dy, dc))
            copy.start()
            ret_copies.append(copy)

    for c in range(len(CHUNKS)):
        select(c)
        if c > 0:
            send_back(c - 1)
        if c == 0:
            for copy in weight_copies[:4]:
                copy.wait()

        def gate_step(n, carry, c=c):
            gate_up(n, 0)
            if c == 0:
                run_events(n, gate_events)
            return carry

        lax.fori_loop(0, full, gate_step, 0)
        if left:
            gate_up_left()
        if c == 0:
            for copy in weight_copies[4:]:
                copy.wait()

        def down_step(n, carry, c=c):
            down(c, n)
            if c == 0:
                run_events(n, down_events)
            return carry

        lax.fori_loop(0, down_tiles, down_step, 0)

    for sems, half, i, count in sends:
        view = rows(me, 0, count)
        remote(view, view, sems.at[half, i], ag_recv.at[0, 0], at_chip(0, 0, 1)).wait_send()
    s_tile = quarter
    s_steps = [(n * s_tile, min(s_tile, sinter - n * s_tile)) for n in range(-(-sinter // s_tile))]
    pair_slots = xall.shape[0] // (2 * dim)
    pairs = []
    for n, (col, width) in enumerate(s_steps):
        top_row = (n % pair_slots) * 2 * dim
        views = [xall.at[pl.ds(top_row + i * dim, dim), pl.ds(0, width)] for i in range(2)]
        pairs.append([
            pltpu.make_async_copy(w.at[:, pl.ds(col, width)], views[i], s_sem.at[2 * (n % pair_slots) + i])
            for i, w in enumerate((sg_hbm, su_hbm))
        ])
    downs = [
        pltpu.make_async_copy(
            sd_hbm.at[:, pl.ds(n * s_tile, s_tile)], xall.at[pl.ds(n * sinter, sinter), :], s_sem.at[2 * pair_slots + n]
        )
        for n in range(4)
    ]
    for n in range(min(pair_slots, len(pairs))):
        for copy in pairs[n]:
            copy.start()
    send_back(len(CHUNKS) - 1)

    started = 0
    for n, (col, width) in enumerate(s_steps):
        for copy in pairs[n]:
            copy.wait()
        top_row = (n % pair_slots) * 2 * dim
        gate = dot(xn[...], xall[top_row : top_row + dim, 0:width])
        up = dot(xn[...], xall[top_row + dim : top_row + 2 * dim, 0:width])
        hs[:, col : col + width] = (jax.nn.silu(gate) * up).astype(BF16)
        if n + pair_slots < len(pairs):
            for copy in pairs[n + pair_slots]:
                copy.start()
        busy = [(m % pair_slots) * 2 * dim for m in range(n + 1, min(n + 1 + pair_slots, len(pairs)))]
        while started < 4 and all(
            (started + 1) * sinter <= b or started * sinter >= b + 2 * dim for b in busy
        ):
            if n + pair_slots < len(pairs):
                break
            downs[started].start()
            started += 1
    for n in range(4):
        downs[n].wait()
        cols = slice(n * s_tile, (n + 1) * s_tile)
        y = dot(hs[...], xall[n * sinter : (n + 1) * sinter, :]).astype(BF16)
        acc[:, cols] = x_ref[:, cols].astype(F32) + y.astype(F32)

    for c in range(len(CHUNKS)):
        loads = []
        weights = []
        slot_no = lax.broadcasted_iota(jnp.int32, (cap, lanes), 0).astype(F32)
        for j in range(per):
            dx, dy, dc = chunk_device(c, j)
            dev = at_chip(-dx, -dy, dc)
            if (dx, dy, dc) == (0, 0, 0):
                ret_copies[0].wait()
            else:
                remote(outb.at[0], recv_hbm.at[dev], ret_send.at[1], ret_recv.at[dev], dev).wait_recv()
            load = pltpu.make_async_copy(recv_hbm.at[dev], xs.at[pl.ds(j * cap, cap)], load_sem.at[j])
            load.start()
            loads.append(load)
            valid = lax.broadcasted_iota(jnp.int32, (1, lanes), 1) < tok
            low = jnp.where(slot_no == meta[dev, 0:1, :], jnp.where(valid, meta[dev, 2:3, :], 0.0), 0.0)
            high = jnp.where(slot_no == meta[dev, 1:2, :], jnp.where(valid, meta[dev, 3:4, :], 0.0), 0.0)
            weights.append(low + high)
        w_all = jnp.concatenate(weights, axis=0).T
        parts = [p[:tok] for p in split3(w_all)]
        for load in loads:
            load.wait()
        for q in range(4):
            cols = slice(q * quarter, (q + 1) * quarter)
            block = xs[:, cols]
            part = dot(parts[0], block) + dot(parts[1], block) + dot(parts[2], block)
            total = acc[:, cols] + part
            if c == len(CHUNKS) - 1:
                out_ref[:, cols] = total.astype(BF16)
            else:
                acc[:, cols] = total

    def meta_sent(k, carry):
        meta_copy(k).wait_send()
        return carry

    lax.fori_loop(1, ep, meta_sent, 0)
    for copy in ret_copies[1:]:
        copy.wait_send()


def solution(mesh):
    ep_size = mesh.shape["ep"]
    side = math.isqrt(ep_size // 2)

    def local_block(hidden_in, norm_gain, router_w, w_gate, w_up, w_down, ws_gate, ws_up, ws_down, expert_ids):
        tok, top_k = expert_ids.shape
        dim = hidden_in.shape[1]
        exp_dev, _, inter = w_gate.shape
        sinter = ws_gate.shape[1]
        cap = GROUPS * ((top_k + GROUP_LIMIT - 1) // GROUP_LIMIT) * tok // ep_size
        lanes = 128
        ids = jnp.pad(expert_ids.T, ((0, 8 - top_k), (0, lanes - tok)), constant_values=-1)
        chunk_rows = cap * 8
        any_spec = pl.BlockSpec(memory_space=pl.ANY)
        vmem_spec = pl.BlockSpec(memory_space=pltpu.VMEM)
        out, _ = pl.pallas_call(
            functools.partial(moe_kernel, side, cap),
            out_shape=(
                jax.ShapeDtypeStruct((tok, dim), BF16),
                jax.ShapeDtypeStruct((ep_size, cap, dim), BF16),
            ),
            in_specs=[vmem_spec] * 4 + [any_spec] * 6,
            out_specs=(vmem_spec, any_spec),
            scratch_shapes=[
                pltpu.VMEM((exp_dev, dim, inter), BF16),
                pltpu.VMEM((exp_dev, dim, inter), BF16),
                pltpu.VMEM((exp_dev * inter, dim), BF16),
                pltpu.VMEM((ep_size * 4 * tok, dim // 4), BF16),
                pltpu.VMEM((tok, dim), BF16),
                pltpu.VMEM((ep_size, cap, dim), BF16),
                pltpu.VMEM((chunk_rows, dim), BF16),
                pltpu.VMEM((chunk_rows, exp_dev * inter), BF16),
                pltpu.VMEM((chunk_rows, 256), F32),
                pltpu.VMEM((tok, dim), F32),
                pltpu.VMEM((tok, sinter), BF16),
                pltpu.VMEM((ep_size, 8, lanes), F32),
                pltpu.VMEM((ep_size, 8, lanes), F32),
                pltpu.SemaphoreType.DMA((6,)),
                pltpu.SemaphoreType.DMA((32,)),
                pltpu.SemaphoreType.DMA((2, 20)),
                pltpu.SemaphoreType.DMA((2, 20)),
                pltpu.SemaphoreType.DMA((2, side * side)),
                pltpu.SemaphoreType.DMA((2, side * side)),
                pltpu.SemaphoreType.DMA((ep_size,)),
                pltpu.SemaphoreType.DMA((ep_size,)),
                pltpu.SemaphoreType.DMA((ep_size,)),
                pltpu.SemaphoreType.DMA((ep_size,)),
                pltpu.SemaphoreType.DMA((8,)),
            ],
            compiler_params=pltpu.CompilerParams(
                collective_id=0, has_side_effects=True, vmem_limit_bytes=67_000_000
            ),
        )(
            hidden_in, norm_gain.reshape(1, dim), router_w, ids, w_gate, w_up,
            w_down.reshape(exp_dev * inter, dim), ws_gate, ws_up, ws_down,
        )
        return out

    row_spec = P(("dp", "ep"), None)
    in_specs = (row_spec, P(), P(), P("ep"), P("ep"), P("ep"), P(), P(), P(), row_spec)
    return jax.shard_map(local_block, mesh=mesh, in_specs=in_specs, out_specs=row_spec, check_vma=False)
```

time: 340 us -> 166 us (0.49); the launches traced: 334 us -> 166 us
  Pallas kernels: 0 us -> 163 us
  waiting for transfers between devices: 147 us -> 0 us
  local copies, waits for them, and re-layouts: 77.5 us -> 3.05 us
  matrix products: 64.2 us -> 0 us
  other arithmetic: 26.3 us -> 0 us
  starting transfers between devices: 18.3 us -> 0 us
    pallas_call x0 -> x1, Pallas kernels: none -> 163 us  [local_block(): pl.pallas_call(functools.partial(moe_kernel, side, cap), out_shape=(jax.S...]
    all_to_all x3 -> x0, waiting for transfers between devices: 147 us -> none  [the longest x1 75.4 us: local_block(): recv_rows = lax.all_to_all(send_rows, 'ep', 0, 0, tiled=True)]
    dot_general x5 -> x0, matrix products: 64.2 us -> none  [the longest x1 28.8 us: expert_stack(): jnp.einsum('eci,eid->ecd', hidden, w_down, preferred_element_type=jnp.flo...]
    gather x10 -> x0, local copies, waits for them, and re-layouts: 56.9 us -> none  [the longest x1 16.5 us: local_block(): jnp.take(recv_rows, buf_row, axis=0, mode='fill', fill_value=0)]
    all_to_all x3 -> x0, starting transfers between devices: 18.3 us -> none  [the longest x1 7.99 us: local_block(): recv_exp = lax.all_to_all(slot_exp, 'ep', 0, 0, tiled=True)]
    select_n x9 -> x0, other arithmetic: 15.2 us -> none  [the longest x2 5.95 us: local_block(): send_rows = jnp.take(x_norm, slot_tok, axis=0, mode='fill', fill_value=0)]
    scatter x3 -> x0, local copies, waits for them, and re-layouts: 14.4 us -> none  [the longest x1 6.18 us: local_block(): jnp.full((recv_cap,), recv_cap, jnp.int32).at[buf_slot]]
    reduce_sum x5 -> x0, other arithmetic: 6.57 us -> none  [the longest x1 5.31 us: local_block(): jnp.sum(gate_vals[:, :, None] * pair_out.astype(jnp.float32), axis=1)]
  transfers between devices with their start and end apart: 3 -> 0, of which waited for: 2 -> 0; matrix products, arithmetic and copies ran while one was open for 12% -> 0% of each run, Pallas kernels for 0% -> 0%
where the time goes in v1:
time: 166 us
  Pallas kernels  163 us (98%)
  local copies, waits for them, and re-layouts  3.05 us (2%)
    pallas_call x1, Pallas kernels, local_block(): pl.pallas_call(functools.partial(moe_kernel, side, cap), out_shape=(jax.S...  163 us

profile of v1, /device:TPU:103, one launch (start us, length us, event | category | flops | bytes accessed | tf_op | source)
XLA Modules:
  0.0 165.7 jit_solution(2504946475527606708)
XLA Ops:
  0.0 1.3 pad.4.ids_ref
  1.3 162.6 %shard_map.100 = (bf16[96,2048]{1,0:T(8,128)(2,1)}, bf16[32,48,2048]{2,1,0:T(8,128)(2,1)}) custom-call(bf16[96,2048]{1,0:T(8,128)(2,1)} %x_ref.1, f32[1,2048]{1,0:T(1,128)} %bitcast.4, f32[64,2048]{1,0:T(8,128)} %router_ref.1, s32[8,128]{1,0:T(8,128)} %pad.4.ids_ref, bf16[2,2048,1408]{2,1,0:T(8,128)(2,1)} %wg_hbm.1, bf16[2,2048,1408]{2,1,0:T(8,128)(2,1)} %wu_hbm.1, ...), custom_call_target="tpu_custom_call" | custom-call | tf_op jit(solution)/shard_map/pallas_call | solution.py:444
  163.9 1.8 %copy.12 = bf16[96,2048]{1,0:T(8,128)(2,1)} copy(bf16[96,2048]{1,0:T(8,128)(2,1)} %get-tuple-element.6) | data formatting | bytes 786432

commit v2 on v1

--- a/solution.py
+++ b/solution.py
@@ -17,10 +17,10 @@
 BF16 = jnp.bfloat16
 LINE = (0, -1, 1, 2)
 CHUNKS = (
-    ((0, 0), (1, 0), (-1, 0), (0, 1)),
-    ((0, -1), (1, 1), (-1, 1), (1, -1)),
-    ((-1, -1), (2, 0), (0, 2), (2, 1)),
-    ((2, -1), (1, 2), (-1, 2), (2, 2)),
+    ((0, 0), (1, 0), (-1, 0), (2, 0)),
+    ((0, -1), (0, 1), (1, -1), (-1, 1)),
+    ((0, 2), (1, 2), (-1, 2), (2, 2)),
+    ((-1, -1), (1, 1), (2, -1), (2, 1)),
 )
 NT = (((1,), (1,)), ((), ()))
 
@@ -58,13 +58,12 @@
     my_x = lax.rem(chip, side)
     my_y = lax.div(chip, side)
 
-    def at_chip(dx, dy, dc=0):
-        col = lax.rem(my_x + (dx + side), side)
-        row = lax.rem(my_y + (dy + side), side)
-        return (row * side + col) * 2 + (lax.rem(core + dc, 2) if dc else core)
-
-    def at(half, da, db, dc=0):
-        return at_chip(da, db, dc) if half == 0 else at_chip(db, da, dc)
+    peer = me + 1 - 2 * core
+
+    def at(first, second, plane=core, dev_core=None):
+        col = lax.rem(my_x + side + second + plane * (first - second), side)
+        row = lax.rem(my_y + side + first + plane * (second - first), side)
+        return (row * side + col) * 2 + (plane if dev_core is None else dev_core)
 
     def rows(src, first, count):
         return xall.at[pl.ds(pl.multiple_of((src * 4 + first) * tok, tok), count * tok)]
@@ -94,6 +93,66 @@
     base = pl.multiple_of(me * 4 * tok, tok)
     for q in range(4):
         xall[pl.ds(pl.multiple_of(base + q * tok, tok), tok), :] = x_norm[:, q * quarter : (q + 1) * quarter]
+
+    pl.semaphore_wait(barrier, ep - 1)
+
+    sends = []
+
+    def remote(src, dst, send_sem, recv_sem, target):
+        return pltpu.make_async_remote_copy(
+            src_ref=src, dst_ref=dst, send_sem=send_sem, recv_sem=recv_sem,
+            device_id={"ep": target}, device_id_type=MESH,
+        )
+
+    def ag_copy(piece, block, first, count, target):
+        view = rows(block, first, count)
+        remote(view, view, ag_send.at[piece], ag_recv.at[piece], target).start()
+        sends.append((ag_send, piece, count))
+
+    def ag_wait(piece, block, first, count):
+        view = rows(block, first, count)
+        remote(view, view, ag_send.at[piece], ag_recv.at[piece], at(1, 0)).wait_recv()
+
+    def swap(first, second):
+        view = rows(at(first, second), 0, 4)
+        slot = (first % side) * side + second % side
+        remote(view, view, d2d_send.at[slot], d2d_recv.at[slot], peer).start()
+        sends.append((d2d_send, slot, 4))
+
+    def second_axis(line):
+        block = at(LINE[line], 0)
+        ag_copy(4 + 2 * line, block, 0, 4, at(0, 1))
+        ag_copy(5 + 2 * line, block, 0, 4, at(0, -1))
+
+    def first_arrived(way):
+        off = (-1, 1)[way]
+        block = at(off, 0)
+        ag_wait(way, block, 0, 4)
+        ag_copy(2 + way, block, 2 * way, 2, at(-off, 0))
+
+    def first_far_arrived():
+        block = at(2, 0)
+        for way in range(2):
+            ag_wait(2 + way, block, 2 * way, 2)
+        swap(2, 0)
+        second_axis(3)
+
+    def second_arrived(line, way):
+        off = (-1, 1)[way]
+        block = at(LINE[line], off)
+        ag_wait(4 + 2 * line + way, block, 0, 4)
+        ag_copy(12 + 2 * line + way, block, 2 * way, 2, at(0, -off))
+        swap(LINE[line], off)
+
+    def second_far_arrived(line):
+        block = at(LINE[line], 2)
+        for way in range(2):
+            ag_wait(12 + 2 * line + way, block, 2 * way, 2)
+        swap(LINE[line], 2)
+
+    ag_copy(0, me, 0, 4, at(1, 0))
+    ag_copy(1, me, 0, 4, at(-1, 0))
+    swap(0, 0)
 
     ids = ids_ref[...]
     expert = lax.broadcasted_iota(jnp.int32, (nexp, lanes), 0)
@@ -120,75 +179,6 @@
         meta[d, 0:2, :] = rank[2 * d : 2 * d + 2, :]
         meta[d, 2:4, 0:tok] = gates[2 * d : 2 * d + 2, :]
 
-    pl.semaphore_wait(barrier, ep - 1)
-
-    sends = []
-
-    def remote(src, dst, send_sem, recv_sem, target):
-        return pltpu.make_async_remote_copy(
-            src_ref=src, dst_ref=dst, send_sem=send_sem, recv_sem=recv_sem,
-            device_id={"ep": target}, device_id_type=MESH,
-        )
-
-    def ag_copy(half, piece, block, first, count, target):
-        remote(
-            rows(block, first, count), rows(block, first, count), ag_send.at[half, piece], ag_recv.at[half, piece], target
-        ).start()
-        sends.append((ag_send, half, piece, count))
-
-    def ag_wait(half, piece, block, first, count):
-        remote(
-            rows(block, first, count), rows(block, first, count), ag_send.at[half, piece], ag_recv.at[half, piece], at(half, 1, 0)
-        ).wait_recv()
-
-    def chip_slot(da, db, half):
-        dx, dy = (da, db) if half == 0 else (db, da)
-        return (dy % side) * side + dx % side
-
-    def swap(half, da, db):
-        block = at(half, da, db)
-        view = rows(block, 2 * half, 2)
-        slot = chip_slot(da, db, half)
-        remote(view, view, d2d_send.at[half, slot], d2d_recv.at[half, slot], at_chip(0, 0, 1)).start()
-        sends.append((d2d_send, half, slot, 2))
-
-    def second_axis(half, line):
-        block = at(half, LINE[line], 0)
-        ag_copy(half, 4 + 2 * line, block, 2 * half, 2, at(half, 0, 1))
-        ag_copy(half, 5 + 2 * line, block, 2 * half, 2, at(half, 0, -1))
-
-    def first_arrived(half, way):
-        off = (-1, 1)[way]
-        block = at(half, off, 0)
-        ag_wait(half, way, block, 2 * half, 2)
-        ag_copy(half, 2 + way, block, 2 * half + way, 1, at(half, -off, 0))
-        second_axis(half, 1 + way)
-        swap(half, off, 0)
-
-    def first_far_arrived(half):
-        block = at(half, 2, 0)
-        for way in range(2):
-            ag_wait(half, 2 + way, block, 2 * half + way, 1)
-        second_axis(half, 3)
-        swap(half, 2, 0)
-
-    def second_arrived(half, line, way):
-        off = (-1, 1)[way]
-        block = at(half, LINE[line], off)
-        ag_wait(half, 4 + 2 * line + way, block, 2 * half, 2)
-        ag_copy(half, 12 + 2 * line + way, block, 2 * half + way, 1, at(half, 0, -off))
-        swap(half, LINE[line], off)
-
-    def second_far_arrived(half, line):
-        block = at(half, LINE[line], 2)
-        for way in range(2):
-            ag_wait(half, 12 + 2 * line + way, block, 2 * half + way, 1)
-        swap(half, LINE[line], 2)
-
-    for half in range(2):
-        ag_copy(half, 0, me, 2 * half, 2, at(half, 1, 0))
-        ag_copy(half, 1, me, 2 * half, 2, at(half, -1, 0))
-
     def meta_copy(k):
         target = lax.rem(me + k, ep)
         return remote(meta.at[target], meta_in.at[me], meta_send.at[k], meta_recv.at[me], target)
@@ -197,43 +187,31 @@
         meta_copy(k).start()
         return carry
 
-    for half in range(2):
-        second_axis(half, 0)
+    first_arrived(0)
+    first_arrived(1)
     lax.fori_loop(1, ep, send_meta, 0)
     own_meta = pltpu.make_async_copy(meta.at[me], meta_in.at[me], meta_recv.at[me])
     own_meta.start()
-    for half in range(2):
-        swap(half, 0, 0)
-    for half in range(2):
-        for way in range(2):
-            first_arrived(half, way)
-    for half in range(2):
-        for way in range(2):
-            second_arrived(half, 0, way)
-
-    def events(*calls):
-        return calls
+    second_axis(0)
+    for way in range(2):
+        swap((-1, 1)[way], 0)
+        second_axis(1 + way)
+    first_far_arrived()
 
     gate_events = (
-        events((first_far_arrived, 0), (first_far_arrived, 1)),
-        events((second_arrived, 0, 1, 0), (second_arrived, 1, 1, 0), (second_arrived, 0, 1, 1), (second_arrived, 1, 1, 1)),
-        events((second_arrived, 0, 2, 0), (second_arrived, 1, 2, 0), (second_arrived, 0, 2, 1), (second_arrived, 1, 2, 1)),
-        events((second_far_arrived, 0, 0), (second_far_arrived, 1, 0)),
-        events((second_arrived, 0, 3, 0), (second_arrived, 1, 3, 0), (second_arrived, 0, 3, 1), (second_arrived, 1, 3, 1)),
+        ((), ((second_arrived, 0, 0), (second_arrived, 0, 1)), ((second_arrived, 1, 0), (second_arrived, 1, 1)), (), ((second_arrived, 2, 0), (second_arrived, 2, 1))),
+        (((second_far_arrived, 0),), ((second_far_arrived, 1),), ((second_far_arrived, 2),), ((second_far_arrived, 3),)),
     )
-    down_events = (
-        events((second_far_arrived, 0, 1), (second_far_arrived, 1, 1)),
-        events((second_far_arrived, 0, 2), (second_far_arrived, 1, 2)),
-        events((second_far_arrived, 0, 3), (second_far_arrived, 1, 3)),
-    )
+    down_events = (((),) * 5 + (((second_arrived, 3, 0), (second_arrived, 3, 1)),), ())
 
     tile = 256
     per = 2 * len(CHUNKS[0])
     full, left = inter // tile, inter % tile
     down_tiles = dim // tile
 
-    def chunk_device(c, j):
-        return (*CHUNKS[c][j // 2], j % 2)
+    def source(c, j):
+        first, second = CHUNKS[c][j % (per // 2)]
+        return at(first, second, core if j < per // 2 else 1 - core)
 
     def wait_meta(src):
         remote(meta.at[0], meta_in.at[src], meta_send.at[1], meta_recv.at[src], src).wait_recv()
@@ -241,17 +219,16 @@
     def select(c):
         slot_no = lax.broadcasted_iota(jnp.int32, (cap, tok), 0).astype(F32)
         for j in range(per):
-            dx, dy, dc = chunk_device(c, j)
-            src = at_chip(dx, dy, dc)
-            if (dx, dy, dc) == (0, 0, 0):
+            src = source(c, j)
+            if c == 0 and j == 0:
                 own_meta.wait()
             else:
                 wait_meta(src)
-            if dc:
-                for half in range(2):
-                    slot = (dy % side) * side + dx % side
-                    view = rows(src, 2 * half, 2)
-                    remote(view, view, d2d_send.at[half, slot], d2d_recv.at[half, slot], at_chip(0, 0, 1)).wait_recv()
+            if j >= per // 2:
+                first, second = CHUNKS[c][j % (per // 2)]
+                slot = (first % side) * side + second % side
+                view = rows(src, 0, 4)
+                remote(view, view, d2d_send.at[slot], d2d_recv.at[slot], peer).wait_recv()
             low = jnp.where(slot_no == meta_in[src, 0:1, 0:tok], 1.0, 0.0)
             high = jnp.where(slot_no == meta_in[src, 1:2, 0:tok], 1.0, 0.0)
             mask[j * cap : (j + 1) * cap, :] = jnp.broadcast_to(jnp.sum(low, axis=1, keepdims=True), (cap, tile))
@@ -297,12 +274,11 @@
 
     def send_back(c):
         for j in range(per):
-            dx, dy, dc = chunk_device(c, j)
             block = outb.at[c * per + j]
-            if (dx, dy, dc) == (0, 0, 0):
+            if c == 0 and j == 0:
                 copy = pltpu.make_async_copy(block, recv_hbm.at[me], ret_recv.at[me])
             else:
-                copy = remote(block, recv_hbm.at[me], ret_send.at[c * per + j], ret_recv.at[me], at_chip(dx, dy, dc))
+                copy = remote(block, recv_hbm.at[me], ret_send.at[c * per + j], ret_recv.at[me], source(c, j))
             copy.start()
             ret_copies.append(copy)
 
@@ -316,8 +292,8 @@
 
         def gate_step(n, carry, c=c):
             gate_up(n, 0)
-            if c == 0:
-                run_events(n, gate_events)
+            if c < len(gate_events):
+                run_events(n, gate_events[c])
             return carry
 
         lax.fori_loop(0, full, gate_step, 0)
@@ -329,15 +305,15 @@
 
         def down_step(n, carry, c=c):
             down(c, n)
-            if c == 0:
-                run_events(n, down_events)
+            if c < len(down_events):
+                run_events(n, down_events[c])
             return carry
 
         lax.fori_loop(0, down_tiles, down_step, 0)
 
-    for sems, half, i, count in sends:
+    for sems, i, count in sends:
         view = rows(me, 0, count)
-        remote(view, view, sems.at[half, i], ag_recv.at[0, 0], at_chip(0, 0, 1)).wait_send()
+        remote(view, view, sems.at[i], ag_recv.at[0], peer).wait_send()
     s_tile = quarter
     s_steps = [(n * s_tile, min(s_tile, sinter - n * s_tile)) for n in range(-(-sinter // s_tile))]
     pair_slots = xall.shape[0] // (2 * dim)
@@ -390,9 +366,9 @@
         weights = []
         slot_no = lax.broadcasted_iota(jnp.int32, (cap, lanes), 0).astype(F32)
         for j in range(per):
-            dx, dy, dc = chunk_device(c, j)
-            dev = at_chip(-dx, -dy, dc)
-            if (dx, dy, dc) == (0, 0, 0):
+            first, second = CHUNKS[c][j % (per // 2)]
+            dev = at(-first, -second, core, core if j < per // 2 else 1 - core)
+            if c == 0 and j == 0:
                 ret_copies[0].wait()
             else:
                 remote(outb.at[0], recv_hbm.at[dev], ret_send.at[1], ret_recv.at[dev], dev).wait_recv()
@@ -465,10 +441,10 @@
                 pltpu.VMEM((ep_size, 8, lanes), F32),
                 pltpu.SemaphoreType.DMA((6,)),
                 pltpu.SemaphoreType.DMA((32,)),
-                pltpu.SemaphoreType.DMA((2, 20)),
-                pltpu.SemaphoreType.DMA((2, 20)),
-                pltpu.SemaphoreType.DMA((2, side * side)),
-                pltpu.SemaphoreType.DMA((2, side * side)),
+                pltpu.SemaphoreType.DMA((20,)),
+                pltpu.SemaphoreType.DMA((20,)),
+                pltpu.SemaphoreType.DMA((side * side,)),
+                pltpu.SemaphoreType.DMA((side * side,)),
                 pltpu.SemaphoreType.DMA((ep_size,)),
                 pltpu.SemaphoreType.DMA((ep_size,)),
                 pltpu.SemaphoreType.DMA((ep_size,)),

time: 166 us -> 146 us (0.88)
  the two profiles are of different devices: /device:TPU:103 before, /device:TPU:101 now
where the time goes in v2:
time: 146 us
  Pallas kernels  143 us (98%)
  local copies, waits for them, and re-layouts  3.05 us (2%)
    pallas_call x1, Pallas kernels, local_block(): pl.pallas_call(functools.partial(moe_kernel, side, cap), out_shape=(jax.S...  143 us

profile of v2, /device:TPU:101, one launch (start us, length us, event | category | flops | bytes accessed | tf_op | source)
XLA Modules:
  0.0 145.6 jit_solution(4237214632133775450)
XLA Ops:
  0.0 1.3 pad.4.ids_ref
  1.3 142.5 %shard_map.100 = (bf16[96,2048]{1,0:T(8,128)(2,1)}, bf16[32,48,2048]{2,1,0:T(8,128)(2,1)}) custom-call(bf16[96,2048]{1,0:T(8,128)(2,1)} %x_ref.1, f32[1,2048]{1,0:T(1,128)} %bitcast.4, f32[64,2048]{1,0:T(8,128)} %router_ref.1, s32[8,128]{1,0:T(8,128)} %pad.4.ids_ref, bf16[2,2048,1408]{2,1,0:T(8,128)(2,1)} %wg_hbm.1, bf16[2,2048,1408]{2,1,0:T(8,128)(2,1)} %wu_hbm.1, ...), custom_call_target="tpu_custom_call" | custom-call | tf_op jit(solution)/shard_map/pallas_call | solution.py:420
  143.8 1.8 %copy.12 = bf16[96,2048]{1,0:T(8,128)(2,1)} copy(bf16[96,2048]{1,0:T(8,128)(2,1)} %get-tuple-element.6) | data formatting | bytes 786432

commit v3 on v2

--- a/solution.py
+++ b/solution.py
@@ -17,10 +17,14 @@
 BF16 = jnp.bfloat16
 LINE = (0, -1, 1, 2)
 CHUNKS = (
-    ((0, 0), (1, 0), (-1, 0), (2, 0)),
-    ((0, -1), (0, 1), (1, -1), (-1, 1)),
-    ((0, 2), (1, 2), (-1, 2), (2, 2)),
-    ((-1, -1), (1, 1), (2, -1), (2, 1)),
+    ((0, 0), (1, 0)),
+    ((-1, 0), (2, 0)),
+    ((-1, -1), (1, 1)),
+    ((2, -1), (2, 1)),
+    ((1, 2), (-1, 2)),
+    ((0, 2), (2, 2)),
+    ((1, -1), (-1, 1)),
+    ((0, -1), (0, 1)),
 )
 NT = (((1,), (1,)), ((), ()))
 
@@ -42,7 +46,7 @@
     side, cap,
     x_ref, gain_ref, router_ref, ids_ref, wg_hbm, wu_hbm, wd_hbm, sg_hbm, su_hbm, sd_hbm,
     out_ref, recv_hbm,
-    wg, wu, wd, xall, xn, outb, xs, h, mask, acc, hs, meta, meta_in,
+    wg, wu, wd, xall, xn, outb, xs, h, mask, acc, hs, mix, meta, meta_in,
     w_sem, s_sem, ag_send, ag_recv, d2d_send, d2d_recv, meta_send, meta_recv, ret_send, ret_recv, load_sem,
 ):
     ep = 2 * side * side
@@ -154,10 +158,12 @@
     ag_copy(1, me, 0, 4, at(-1, 0))
     swap(0, 0)
 
-    ids = ids_ref[...]
-    expert = lax.broadcasted_iota(jnp.int32, (nexp, lanes), 0)
+    top = ids_ref.shape[1]
+    unit = lax.broadcasted_iota(jnp.int32, (8, top), 0) == lax.broadcasted_iota(jnp.int32, (8, top), 1)
+    ids = dot(jnp.where(unit, 1.0, 0.0).astype(BF16), ids_ref[...].astype(F32).astype(BF16), NT)
+    ids = jnp.concatenate([ids, jnp.full((8, lanes - tok), -1.0, F32)], axis=1)
+    expert = lax.broadcasted_iota(jnp.int32, (nexp, lanes), 0).astype(F32)
     hot = expert == ids[0:1, :]
-    top = 6
     for k in range(1, top):
         hot = jnp.logical_or(hot, expert == ids[k : k + 1, :])
     hot = jnp.where(hot, 1.0, 0.0)
@@ -199,10 +205,15 @@
     first_far_arrived()
 
     gate_events = (
-        ((), ((second_arrived, 0, 0), (second_arrived, 0, 1)), ((second_arrived, 1, 0), (second_arrived, 1, 1)), (), ((second_arrived, 2, 0), (second_arrived, 2, 1))),
-        (((second_far_arrived, 0),), ((second_far_arrived, 1),), ((second_far_arrived, 2),), ((second_far_arrived, 3),)),
+        ((), ((second_arrived, 0, 0), (second_arrived, 0, 1)), (), (), ((second_arrived, 1, 0), (second_arrived, 1, 1))),
+        ((), ((second_arrived, 2, 0), (second_arrived, 2, 1)), (), (), ()),
+        ((), ((second_far_arrived, 0),), (), (), ((second_far_arrived, 1),)),
     )
-    down_events = (((),) * 5 + (((second_arrived, 3, 0), (second_arrived, 3, 1)),), ())
+    down_events = (
+        (),
+        ((), ((second_arrived, 3, 0), (second_arrived, 3, 1))),
+        ((), ((second_far_arrived, 2),), (), (), (), ((second_far_arrived, 3),)),
+    )
 
     tile = 256
     per = 2 * len(CHUNKS[0])
@@ -361,13 +372,26 @@
         y = dot(hs[...], xall[n * sinter : (n + 1) * sinter, :]).astype(BF16)
         acc[:, cols] = x_ref[:, cols].astype(F32) + y.astype(F32)
 
+    slot_no = lax.broadcasted_iota(jnp.int32, (cap, lanes), 0).astype(F32)
+    valid = lax.broadcasted_iota(jnp.int32, (1, lanes), 1) < tok
     for c in range(len(CHUNKS)):
         loads = []
         weights = []
-        slot_no = lax.broadcasted_iota(jnp.int32, (cap, lanes), 0).astype(F32)
+
+        def worker(j, c=c):
+            first, second = CHUNKS[c][j % (per // 2)]
+            return at(-first, -second, core, core if j < per // 2 else 1 - core)
+
         for j in range(per):
-            first, second = CHUNKS[c][j % (per // 2)]
-            dev = at(-first, -second, core, core if j < per // 2 else 1 - core)
+            dev = worker(j)
+            low = jnp.where(slot_no == meta[dev, 0:1, :], jnp.where(valid, meta[dev, 2:3, :], 0.0), 0.0)
+            high = jnp.where(slot_no == meta[dev, 1:2, :], jnp.where(valid, meta[dev, 3:4, :], 0.0), 0.0)
+            weights.append(low + high)
+        w_all = jnp.concatenate(weights, axis=0).T
+        for i, part in enumerate(split3(w_all)):
+            mix[i * tok : (i + 1) * tok, :] = part[:tok]
+        for j in range(per):
+            dev = worker(j)
             if c == 0 and j == 0:
                 ret_copies[0].wait()
             else:
@@ -375,19 +399,13 @@
             load = pltpu.make_async_copy(recv_hbm.at[dev], xs.at[pl.ds(j * cap, cap)], load_sem.at[j])
             load.start()
             loads.append(load)
-            valid = lax.broadcasted_iota(jnp.int32, (1, lanes), 1) < tok
-            low = jnp.where(slot_no == meta[dev, 0:1, :], jnp.where(valid, meta[dev, 2:3, :], 0.0), 0.0)
-            high = jnp.where(slot_no == meta[dev, 1:2, :], jnp.where(valid, meta[dev, 3:4, :], 0.0), 0.0)
-            weights.append(low + high)
-        w_all = jnp.concatenate(weights, axis=0).T
-        parts = [p[:tok] for p in split3(w_all)]
         for load in loads:
             load.wait()
         for q in range(4):
             cols = slice(q * quarter, (q + 1) * quarter)
             block = xs[:, cols]
-            part = dot(parts[0], block) + dot(parts[1], block) + dot(parts[2], block)
-            total = acc[:, cols] + part
+            part = dot(mix[...], block)
+            total = acc[:, cols] + (part[:tok] + part[tok : 2 * tok] + part[2 * tok :])
             if c == len(CHUNKS) - 1:
                 out_ref[:, cols] = total.astype(BF16)
             else:
@@ -413,8 +431,7 @@
         sinter = ws_gate.shape[1]
         cap = GROUPS * ((top_k + GROUP_LIMIT - 1) // GROUP_LIMIT) * tok // ep_size
         lanes = 128
-        ids = jnp.pad(expert_ids.T, ((0, 8 - top_k), (0, lanes - tok)), constant_values=-1)
-        chunk_rows = cap * 8
+        chunk_rows = cap * 2 * len(CHUNKS[0])
         any_spec = pl.BlockSpec(memory_space=pl.ANY)
         vmem_spec = pl.BlockSpec(memory_space=pltpu.VMEM)
         out, _ = pl.pallas_call(
@@ -437,6 +454,7 @@
                 pltpu.VMEM((chunk_rows, 256), F32),
                 pltpu.VMEM((tok, dim), F32),
                 pltpu.VMEM((tok, sinter), BF16),
+                pltpu.VMEM((3 * tok, chunk_rows), BF16),
                 pltpu.VMEM((ep_size, 8, lanes), F32),
                 pltpu.VMEM((ep_size, 8, lanes), F32),
                 pltpu.SemaphoreType.DMA((6,)),
@@ -455,7 +473,7 @@
                 collective_id=0, has_side_effects=True, vmem_limit_bytes=67_000_000
             ),
         )(
-            hidden_in, norm_gain.reshape(1, dim), router_w, ids, w_gate, w_up,
+            hidden_in, norm_gain.reshape(1, dim), router_w, expert_ids, w_gate, w_up,
             w_down.reshape(exp_dev * inter, dim), ws_gate, ws_up, ws_down,
         )
         return out

time: 146 us -> 139 us (0.952)
  the two profiles are of different devices: /device:TPU:101 before, /device:TPU:103 now
where the time goes in v3:
time: 139 us; the launch traced here: 137 us
  Pallas kernels  134 us (96%)
  local copies, waits for them, and re-layouts  3.17 us (2%)
    pallas_call x1, Pallas kernels, local_block(): pl.pallas_call(functools.partial(moe_kernel, side, cap), out_shape=(jax.S...  134 us
    unnamed x2, local copies, waits for them, and re-layouts  3.17 us

profile of v3, /device:TPU:103, one launch (start us, length us, event | category | flops | bytes accessed | tf_op | source)
XLA Modules:
  0.0 136.9 jit_solution(3963216270098399254)
XLA Ops:
  0.0 1.4 %copy.11.ids_ref = s32[96,6]{1,0:T(8,128)} copy(s32[96,6]{0,1:T(8,128)} %param.19) | data formatting | bytes 4608 | tf_op args[9]
  1.4 133.7 %shard_map.100 = (bf16[96,2048]{1,0:T(8,128)(2,1)}, bf16[32,48,2048]{2,1,0:T(8,128)(2,1)}) custom-call(bf16[96,2048]{1,0:T(8,128)(2,1)} %x_ref.1, f32[1,2048]{1,0:T(1,128)} %bitcast.3, f32[64,2048]{1,0:T(8,128)} %router_ref.1, s32[96,6]{1,0:T(8,128)} %copy.11.ids_ref, bf16[2,2048,1408]{2,1,0:T(8,128)(2,1)} %wg_hbm.1, bf16[2,2048,1408]{2,1,0:T(8,128)(2,1)} %wu_hbm.1, ...), custom_call_target="tpu_custom_call" | custom-call | tf_op jit(solution)/shard_map/pallas_call | solution.py:437
  135.1 1.8 %copy.13 = bf16[96,2048]{1,0:T(8,128)(2,1)} copy(bf16[96,2048]{1,0:T(8,128)(2,1)} %get-tuple-element.6) | data formatting | bytes 786432

commit v4 on v3

--- a/solution.py
+++ b/solution.py
@@ -202,10 +202,9 @@
     for way in range(2):
         swap((-1, 1)[way], 0)
         second_axis(1 + way)
-    first_far_arrived()
 
     gate_events = (
-        ((), ((second_arrived, 0, 0), (second_arrived, 0, 1)), (), (), ((second_arrived, 1, 0), (second_arrived, 1, 1))),
+        (((first_far_arrived,),), (), ((second_arrived, 0, 0), (second_arrived, 0, 1)), (), ((second_arrived, 1, 0), (second_arrived, 1, 1))),
         ((), ((second_arrived, 2, 0), (second_arrived, 2, 1)), (), (), ()),
         ((), ((second_far_arrived, 0),), (), (), ((second_far_arrived, 1),)),
     )

time: 139 us -> 139 us (level)
  no operation moved by 1% of the time
where the time goes in v4:
time: 139 us; the launch traced here: 137 us
  Pallas kernels  134 us (96%)
  local copies, waits for them, and re-layouts  3.17 us (2%)
    pallas_call x1, Pallas kernels, local_block(): pl.pallas_call(functools.partial(moe_kernel, side, cap), out_shape=(jax.S...  134 us
    unnamed x2, local copies, waits for them, and re-layouts  3.17 us

profile of v4, /device:TPU:103, one launch (start us, length us, event | category | flops | bytes accessed | tf_op | source)
XLA Modules:
  0.0 136.9 jit_solution(2021418402923375706)
XLA Ops:
  0.0 1.4 %copy.11.ids_ref = s32[96,6]{1,0:T(8,128)} copy(s32[96,6]{0,1:T(8,128)} %param.19) | data formatting | bytes 4608 | tf_op args[9]
  1.4 133.7 %shard_map.100 = (bf16[96,2048]{1,0:T(8,128)(2,1)}, bf16[32,48,2048]{2,1,0:T(8,128)(2,1)}) custom-call(bf16[96,2048]{1,0:T(8,128)(2,1)} %x_ref.1, f32[1,2048]{1,0:T(1,128)} %bitcast.3, f32[64,2048]{1,0:T(8,128)} %router_ref.1, s32[96,6]{1,0:T(8,128)} %copy.11.ids_ref, bf16[2,2048,1408]{2,1,0:T(8,128)(2,1)} %wg_hbm.1, bf16[2,2048,1408]{2,1,0:T(8,128)(2,1)} %wu_hbm.1, ...), custom_call_target="tpu_custom_call" | custom-call | tf_op jit(solution)/shard_map/pallas_call | solution.py:436
  135.1 1.8 %copy.13 = bf16[96,2048]{1,0:T(8,128)(2,1)} copy(bf16[96,2048]{1,0:T(8,128)(2,1)} %get-tuple-element.6) | data formatting | bytes 786432
